TPU v7x, 32 devices: a whole 2x2x4 slice. The times are simulated.
32 devices in a mesh: dp: 8 (over z, y), tensor: 4 (over x, core).
Axes of the slice: x: 2, y: 2, z: 4, core: 2. Of those that a mesh axis runs over, the one named last changes fastest.
Arguments:
- block_input: bfloat16 [2, 1024, 8, 1024], P(None, 'tensor', 'dp'), may hold values from -6 to 6
- qkv_weight: bfloat16 [1024, 3, 1024], P('dp', None, 'tensor'), may hold values from -0.1875 to 0.1875
- qv_bias: float32 [2, 1024], P(None, 'tensor'), may hold values from -2 to 2
- out_weight: bfloat16 [1024, 1024], P('dp', 'tensor'), may hold values from -0.75 to 0.75
- out_bias: float32 [1024], replicated, may hold values from -2 to 2
- fc_weight: bfloat16 [1024, 4096], P('dp', 'tensor'), may hold values from -0.1875 to 0.1875
- fc_bias: float32 [4096], P('tensor'), may hold values from -2 to 2
- proj_weight: bfloat16 [1024, 4096], P('dp', 'tensor'), may hold values from -0.09375 to 0.09375
- proj_bias: float32 [1024], replicated, may hold values from -2 to 2
- norm1_gain: float32 [1024], replicated, may hold values from 0.1 to 1.9
- norm1_shift: float32 [1024], replicated, may hold values from -2 to 2
- norm2_gain: float32 [1024], replicated, may hold values from 0.1 to 1.9
- norm2_shift: float32 [1024], replicated, may hold values from -2 to 2
- out_grad: bfloat16 [2, 1024, 8, 1024], P(None, 'tensor', 'dp'), may hold values from -6 to 6
Outputs:
- block_output: bfloat16 [2, 1024, 8, 1024], P(None, 'tensor', 'dp')
- input_grad: bfloat16 [2, 1024, 8, 1024], P(None, 'tensor', 'dp')
- qkv_weight_grad: float32 [1024, 3, 1024], P('dp', None, 'tensor')
- qv_bias_grad: float32 [2, 1024], P(None, 'tensor')
- out_weight_grad: float32 [1024, 1024], P('dp', 'tensor')
- out_bias_grad: float32 [1024], replicated
- fc_weight_grad: float32 [1024, 4096], P('dp', 'tensor')
- fc_bias_grad: float32 [4096], P('tensor')
- proj_weight_grad: float32 [1024, 4096], P('dp', 'tensor')
- proj_bias_grad: float32 [1024], replicated
- norm1_gain_grad: float32 [1024], replicated
- norm1_shift_grad: float32 [1024], replicated
- norm2_gain_grad: float32 [1024], replicated
- norm2_shift_grad: float32 [1024], replicated
All inputs are finite; a program needn't handle non-finite values.
Results may differ from a plain program's by a relative error of at most 0.012.
Values may be sent and summed in bfloat16 or wider, within the bound.
A program may use at most 128 MiB of HBM per device.

v0:
```python
import jax
import jax.numpy as jnp
from jax import lax
from jax.sharding import PartitionSpec as P

HEAD_DIM = 64
norm_eps = 1e-05
tanh_coef = 0.7978845608028654
cube_coef = 0.044715
block_rows = 512


def gelu_tanh(values):
    return (
        0.5 * values * (1.0 + jnp.tanh(tanh_coef * (values + cube_coef * values * values * values)))
    )


def norm_parts(rows):
    center = rows - jnp.mean(rows, axis=-1, keepdims=True)
    spread = jnp.mean(center * center, axis=-1, keepdims=True)
    inverse = lax.rsqrt(spread + norm_eps)
    return (center * inverse, inverse)


def norm_back(grad_out, normed, inverse, gain):
    grad_normed = grad_out * gain
    first = jnp.mean(grad_normed, axis=-1, keepdims=True)
    second = jnp.mean(grad_normed * normed, axis=-1, keepdims=True)
    return inverse * (grad_normed - first - normed * second)


def causal_scores(query_block, keys, offset):
    scores = jnp.einsum(
        "qbhe,kbhe->bhqk", query_block, keys, preferred_element_type=jnp.float32
    ) * HEAD_DIM ** (-0.5)
    height = query_block.shape[0]
    length = keys.shape[0]
    row_pos = lax.broadcasted_iota(jnp.int32, (height, length), 0) + offset
    col_pos = lax.broadcasted_iota(jnp.int32, (height, length), 1)
    return jnp.where(col_pos <= row_pos, scores, -1e30)


def attend_forward(queries, keys, values):
    length = keys.shape[0]
    span = min(block_rows, length)
    outputs = []
    totals = []
    for offset in range(0, length, span):
        scores = causal_scores(queries[offset : offset + span], keys, offset)
        peak = jnp.max(scores, axis=-1, keepdims=True)
        raised = jnp.exp(scores - peak)
        total = jnp.sum(raised, axis=-1, keepdims=True)
        weights = (raised / total).astype(jnp.bfloat16)
        outputs.append(
            jnp.einsum("bhqk,kbhe->qbhe", weights, values, preferred_element_type=jnp.float32)
        )
        totals.append(peak + jnp.log(total))
    return (jnp.concatenate(outputs, 0), jnp.concatenate(totals, 2))


def attend_backward(queries, keys, values, log_totals, grad_out):
    length = keys.shape[0]
    span = min(block_rows, length)
    scale = HEAD_DIM ** (-0.5)
    grad_queries = []
    grad_keys = jnp.zeros(keys.shape, jnp.float32)
    grad_values = jnp.zeros(values.shape, jnp.float32)
    for offset in range(0, length, span):
        query_block = queries[offset : offset + span]
        grad_block = grad_out[offset : offset + span]
        scores = causal_scores(query_block, keys, offset)
        probs = jnp.exp(scores - log_totals[:, :, offset : offset + span])
        grad_probs = jnp.einsum(
            "qbhe,kbhe->bhqk", grad_block, values, preferred_element_type=jnp.float32
        )
        inner = jnp.sum(probs * grad_probs, axis=-1, keepdims=True)
        grad_scores = (probs * (grad_probs - inner)).astype(jnp.bfloat16)
        grad_queries.append(
            jnp.einsum("bhqk,kbhe->qbhe", grad_scores, keys, preferred_element_type=jnp.float32)
            * scale
        )
        grad_keys = (
            grad_keys
            + jnp.einsum(
                "bhqk,qbhe->kbhe", grad_scores, query_block, preferred_element_type=jnp.float32
            )
            * scale
        )
        grad_values = grad_values + jnp.einsum(
            "bhqk,qbhe->kbhe",
            probs.astype(jnp.bfloat16),
            grad_block,
            preferred_element_type=jnp.float32,
        )
    return (jnp.concatenate(grad_queries, 0), grad_keys, grad_values)


def per_device(
    block_input,
    qkv_weight,
    qv_bias,
    out_weight,
    out_bias,
    fc_weight,
    fc_bias,
    proj_weight,
    proj_bias,
    norm1_gain,
    norm1_shift,
    norm2_gain,
    norm2_shift,
    out_grad,
):
    micro = block_input.shape[0]
    heads_local = qkv_weight.shape[2] // HEAD_DIM
    rows = qkv_weight.shape[0]
    width_qkv = qkv_weight.shape[1] * qkv_weight.shape[2]
    width_out = out_weight.shape[1]
    width_fc = fc_weight.shape[1]
    cuts = (width_qkv, width_qkv + width_out, width_qkv + width_out + width_fc)
    packed = jnp.concatenate(
        [qkv_weight.reshape(rows, width_qkv), out_weight, fc_weight, proj_weight], axis=1
    )
    packed_full = lax.all_gather(packed, "dp", axis=0, tiled=True)
    depth = packed_full.shape[0]
    qkv_full = packed_full[:, : cuts[0]].reshape(depth, 3, qkv_weight.shape[2])
    out_full = packed_full[:, cuts[0] : cuts[1]]
    fc_full = packed_full[:, cuts[1] : cuts[2]]
    proj_full = packed_full[:, cuts[2] :]
    grad_top_all = lax.all_gather(out_grad, "tensor", axis=1, tiled=True)
    weight_init = jnp.zeros(packed_full.shape, jnp.float32)
    small_init = (
        jnp.zeros(qv_bias.shape, jnp.float32),
        jnp.zeros(fc_bias.shape, jnp.float32),
        jnp.zeros(out_bias.shape, jnp.float32),
        jnp.zeros(proj_bias.shape, jnp.float32),
        jnp.zeros(norm1_gain.shape, jnp.float32),
        jnp.zeros(norm1_shift.shape, jnp.float32),
        jnp.zeros(norm2_gain.shape, jnp.float32),
        jnp.zeros(norm2_shift.shape, jnp.float32),
    )
    outputs_init = jnp.zeros(block_input.shape, jnp.bfloat16)
    in_grads_init = jnp.zeros(block_input.shape, jnp.bfloat16)

    def one_micro(index, carry):
        outputs_all, in_grads_all, weight_acc, small_acc = carry
        resid_in = lax.dynamic_index_in_dim(block_input, index, 0, keepdims=False).astype(
            jnp.float32
        )
        grad_top = lax.dynamic_index_in_dim(out_grad, index, 0, keepdims=False)
        grad_top_full = lax.dynamic_index_in_dim(grad_top_all, index, 0, keepdims=False)
        normed1, inverse1 = norm_parts(resid_in)
        hidden1 = (normed1 * norm1_gain + norm1_shift).astype(jnp.bfloat16)
        hidden1_full = lax.all_gather(hidden1, "tensor", axis=0, tiled=True)
        length = hidden1_full.shape[0]
        batch = hidden1_full.shape[1]
        projected = jnp.einsum(
            "lbd,dce->lbce", hidden1_full, qkv_full, preferred_element_type=jnp.float32
        )
        qkv_bias = jnp.stack([qv_bias[0], jnp.zeros_like(qv_bias[0]), qv_bias[1]])
        qkv_values = (projected + qkv_bias).astype(jnp.bfloat16)
        split = qkv_values.reshape(length, batch, 3, heads_local, HEAD_DIM)
        queries = split[:, :, 0]
        keys = split[:, :, 1]
        values = split[:, :, 2]
        attended, log_totals = attend_forward(queries, keys, values)
        mixed = attended.astype(jnp.bfloat16).reshape(length, batch, heads_local * HEAD_DIM)
        attn_branch = lax.psum_scatter(
            jnp.einsum("lbi,oi->lbo", mixed, out_full, preferred_element_type=jnp.float32),
            "tensor",
            scatter_dimension=0,
            tiled=True,
        )
        middle = resid_in + attn_branch + out_bias
        normed2, inverse2 = norm_parts(middle)
        hidden2 = (normed2 * norm2_gain + norm2_shift).astype(jnp.bfloat16)
        hidden2_full = lax.all_gather(hidden2, "tensor", axis=0, tiled=True)
        pre_act = (
            jnp.einsum("lbd,df->lbf", hidden2_full, fc_full, preferred_element_type=jnp.float32)
            + fc_bias
        )
        activated = gelu_tanh(pre_act).astype(jnp.bfloat16)
        mlp_branch = lax.psum_scatter(
            jnp.einsum(
                "lbf,of->lbo", activated, proj_full, preferred_element_type=jnp.float32
            ).astype(jnp.bfloat16),
            "tensor",
            scatter_dimension=0,
            tiled=True,
        ).astype(jnp.float32)
        block_out = (middle + mlp_branch + proj_bias).astype(jnp.bfloat16)
        grad_proj = jnp.einsum(
            "lbo,lbf->of", grad_top_full, activated, preferred_element_type=jnp.float32
        )
        grad_act = jnp.einsum(
            "lbo,of->lbf", grad_top_full, proj_full, preferred_element_type=jnp.float32
        )
        _, gelu_pull = jax.vjp(gelu_tanh, pre_act)
        grad_pre = gelu_pull(grad_act)[0].astype(jnp.bfloat16)
        grad_fc_bias = jnp.sum(grad_pre.astype(jnp.float32), axis=(0, 1))
        grad_fc = jnp.einsum(
            "lbd,lbf->df", hidden2_full, grad_pre, preferred_element_type=jnp.float32
        )
        grad_h2 = lax.psum_scatter(
            jnp.einsum("lbf,df->lbd", grad_pre, fc_full, preferred_element_type=jnp.float32),
            "tensor",
            scatter_dimension=0,
            tiled=True,
        )
        grad_gain2 = jnp.sum(grad_h2 * normed2, axis=(0, 1))
        grad_shift2 = jnp.sum(grad_h2, axis=(0, 1))
        grad_mid = grad_top.astype(jnp.float32) + norm_back(grad_h2, normed2, inverse2, norm2_gain)
        grad_out_bias = jnp.sum(grad_mid, axis=(0, 1))
        grad_proj_bias = jnp.sum(grad_top.astype(jnp.float32), axis=(0, 1))
        grad_mid_full = lax.all_gather(grad_mid.astype(jnp.bfloat16), "tensor", axis=0, tiled=True)
        grad_out_w = jnp.einsum(
            "lbo,lbi->oi", grad_mid_full, mixed, preferred_element_type=jnp.float32
        )
        grad_mixed = jnp.einsum(
            "lbo,oi->lbi", grad_mid_full, out_full, preferred_element_type=jnp.float32
        )
        grad_mixed = grad_mixed.astype(jnp.bfloat16).reshape(length, batch, heads_local, HEAD_DIM)
        grad_queries, grad_keys, grad_values = attend_backward(
            queries, keys, values, log_totals, grad_mixed
        )
        grad_qkv = jnp.stack([grad_queries, grad_keys, grad_values], axis=2).astype(jnp.bfloat16)
        grad_qkv = grad_qkv.reshape(length, batch, 3, heads_local * HEAD_DIM)
        kind_sums = jnp.sum(grad_qkv.astype(jnp.float32), axis=(0, 1))
        grad_qv_bias = jnp.stack([kind_sums[0], kind_sums[2]])
        grad_qkv_w = jnp.einsum(
            "lbd,lbce->dce", hidden1_full, grad_qkv, preferred_element_type=jnp.float32
        )
        grad_h1 = lax.psum_scatter(
            jnp.einsum("lbce,dce->lbd", grad_qkv, qkv_full, preferred_element_type=jnp.float32),
            "tensor",
            scatter_dimension=0,
            tiled=True,
        )
        grad_gain1 = jnp.sum(grad_h1 * normed1, axis=(0, 1))
        grad_shift1 = jnp.sum(grad_h1, axis=(0, 1))
        grad_in = (grad_mid + norm_back(grad_h1, normed1, inverse1, norm1_gain)).astype(
            jnp.bfloat16
        )
        fresh_weights = jnp.concatenate(
            [grad_qkv_w.reshape(depth, width_qkv), grad_out_w, grad_fc, grad_proj], axis=1
        )
        weight_acc = weight_acc + fresh_weights
        fresh = (
            grad_qv_bias,
            grad_fc_bias,
            grad_out_bias,
            grad_proj_bias,
            grad_gain1,
            grad_shift1,
            grad_gain2,
            grad_shift2,
        )
        small_acc = tuple((total + extra for total, extra in zip(small_acc, fresh)))
        outputs_all = lax.dynamic_update_index_in_dim(outputs_all, block_out, index, 0)
        in_grads_all = lax.dynamic_update_index_in_dim(in_grads_all, grad_in, index, 0)
        return (outputs_all, in_grads_all, weight_acc, small_acc)

    outputs_all, in_grads_all, weight_acc, small_acc = lax.fori_loop(
        0, micro, one_micro, (outputs_init, in_grads_init, weight_init, small_init)
    )
    weight_shard = lax.psum_scatter(weight_acc, "dp", scatter_dimension=0, tiled=True)
    grad_qkv_w = weight_shard[:, : cuts[0]].reshape(qkv_weight.shape)
    grad_out_w = weight_shard[:, cuts[0] : cuts[1]]
    grad_fc_w = weight_shard[:, cuts[1] : cuts[2]]
    grad_proj_w = weight_shard[:, cuts[2] :]
    tensor_size = lax.psum(1, "tensor")
    slot = lax.axis_index("tensor")
    head_vec = jnp.concatenate([small_acc[0].reshape(-1), small_acc[1]])
    head_slots = jnp.zeros((tensor_size, head_vec.shape[0]), jnp.float32)
    head_slots = lax.dynamic_update_index_in_dim(head_slots, head_vec, slot, 0)
    feature_vec = jnp.concatenate([item for item in small_acc[2:]])
    total = lax.psum(jnp.concatenate([feature_vec, head_slots.reshape(-1)]), ("dp", "tensor"))
    features = total[: feature_vec.shape[0]].reshape(6, -1)
    head_total = lax.dynamic_index_in_dim(
        total[feature_vec.shape[0] :].reshape(tensor_size, -1), slot, 0, keepdims=False
    )
    qv_size = small_acc[0].size
    grad_qv_bias = head_total[:qv_size].reshape(small_acc[0].shape)
    grad_fc_bias = head_total[qv_size:]
    return (
        outputs_all,
        in_grads_all,
        grad_qkv_w,
        grad_qv_bias,
        grad_out_w,
        features[0],
        grad_fc_w,
        grad_fc_bias,
        grad_proj_w,
        features[1],
        features[2],
        features[3],
        features[4],
        features[5],
    )


def solution(mesh):
    in_specs = (
        P(None, "tensor", "dp", None),
        P("dp", None, "tensor"),
        P(None, "tensor"),
        P("dp", "tensor"),
        P(),
        P("dp", "tensor"),
        P("tensor"),
        P("dp", "tensor"),
        P(),
        P(),
        P(),
        P(),
        P(),
        P(None, "tensor", "dp", None),
    )
    out_specs = (
        P(None, "tensor", "dp", None),
        P(None, "tensor", "dp", None),
        P("dp", None, "tensor"),
        P(None, "tensor"),
        P("dp", "tensor"),
        P(),
        P("dp", "tensor"),
        P("tensor"),
        P("dp", "tensor"),
        P(),
        P(),
        P(),
        P(),
        P(),
    )
    return jax.shard_map(
        per_device, mesh=mesh, in_specs=in_specs, out_specs=out_specs, check_vma=False
    )
```

profile of v0, /device:TPU:0, one launch (start us, length us, event | category | flops | bytes accessed | tf_op | source)
XLA Modules:
  0.0 999.4 jit_solution(10423390227295797122)
XLA Ops:
  13.4 101.5 %all-gather.6.cloned.1.call-done = bf16[1024,3072]{0,1:T(8,128)(2,1)} async-done(((bf16[128,3072]{0,1:T(8,128)(2,1)}), bf16[1024,3072]{0,1:T(8,128)(2,1)}) %all-gather.6.cloned.1.call-update) | async-done | bytes 6291472 | tf_op jit(solution)/shard_map/all_gather | solution.py:125
  130.1 19.0 %all-gather.8.cloned.1.call-done = bf16[2,1024,1,1024]{3,1,2,0:T(8,128)(2,1)} async-done(((bf16[2,256,1,1024]{3,1,2,0:T(8,128)(2,1)}), bf16[2,1024,1,1024]{3,1,2,0:T(8,128)(2,1)}) %all-gather.8.cloned.1.call-update) | async-done | bytes 4194320 | tf_op jit(solution)/shard_map/all_gather | solution.py:131
  149.1 623.7 %while.34 = (s32[]{:T(128)}, bf16[2,256,1,1024]{3,1,2,0:T(8,128)(2,1)}, bf16[2,256,1,1024]{3,1,2,0:T(8,128)(2,1)}, f32[1024,3072]{0,1:T(8,128)}, f32[2,256]{1,0:...) while((s32[]{:T(128)}, ...), condition=%wide.region_27.28_spmd.clone, body=%wide.region_0.27_spmd.clone.sunk | while | flops 22718711808 | bytes 744419392 | solution.py:264
  151.7 23.2 %all-gather.10.cloned.1.call-done = bf16[1024,1,1024]{2,0,1:T(8,128)(2,1)} async-done(((bf16[256,1,1024]{2,0,1:T(8,128)(2,1)}), bf16[1024,1,1024]{2,0,1:T(8,128)(2,1)}) %all-gather.10.cloned.1.call-update) | async-done | bytes 2097168 | tf_op jit(solution)/shard_map/while/body/eval_jaxpr/all_gather | solution.py:155
  196.7 44.7 %reduce-scatter.8.cloned.1.call-done = f32[256,1,1024]{2,0,1:T(8,128)} async-done(((f32[1024,1,1024]{2,0,1:T(8,128)}), f32[256,1,1024]{2,0,1:T(8,128)}) %reduce-scatter.8.cloned.1.call-update) | async-done | bytes 1048592 | tf_op jit(solution)/shard_map/while/body/eval_jaxpr/reduce_scatter | solution.py:169
  244.5 22.4 %all-gather.12.cloned.1.call-done = bf16[1024,1,1024]{2,0,1:T(8,128)(2,1)} async-done(((bf16[256,1,1024]{2,0,1:T(8,128)(2,1)}), bf16[1024,1,1024]{2,0,1:T(8,128)(2,1)}) %all-gather.12.cloned.1.call-update) | async-done | bytes 2097168 | tf_op jit(solution)/shard_map/while/body/eval_jaxpr/all_gather | solution.py:178
  271.6 5.7 convert_reduce_fusion.9
  283.1 44.7 %reduce-scatter.12.cloned.1.call-done = f32[256,1,1024]{2,0,1:T(8,128)} async-done(((f32[1024,1,1024]{2,0,1:T(8,128)}), f32[256,1,1024]{2,0,1:T(8,128)}) %reduce-scatter.12.cloned.1.call-update) | async-done | bytes 1048592 | tf_op jit(solution)/shard_map/while/body/eval_jaxpr/reduce_scatter | solution.py:205
  332.3 7.0 convert_bitcast_fusion.4
  339.8 15.1 %all-gather.14.cloned.1.call-done = bf16[1024,1,1024]{2,0,1:T(8,128)(2,1)} async-done(((bf16[256,1,1024]{2,0,1:T(8,128)(2,1)}), bf16[1024,1,1024]{2,0,1:T(8,128)(2,1)}) %all-gather.14.cloned.1.call-update) | async-done | bytes 2097168 | tf_op jit(solution)/shard_map/while/body/eval_jaxpr/all_gather | solution.py:216
  362.4 7.6 multiply_reduce_fusion.13
  374.6 6.8 multiply_convert_fusion.11
  384.3 5.5 multiply_reduce_fusion.14
  405.1 5.7 convolution_bitcast_fusion.8
  411.9 6.7 fusion.227
  438.5 5.7 maximum_add_fusion.4
  444.2 11.6 %reduce-scatter.14.cloned.1.call-done = f32[256,1,1024]{2,0,1:T(8,128)} async-done(((f32[1024,1,1024]{2,0,1:T(8,128)}), f32[256,1,1024]{2,0,1:T(8,128)}) %reduce-scatter.14.cloned.1.call-update) | async-done | bytes 1048592 | tf_op jit(solution)/shard_map/while/body/eval_jaxpr/reduce_scatter | solution.py:234
  462.6 22.9 %all-gather.10.cloned.1.call-done = bf16[1024,1,1024]{2,0,1:T(8,128)(2,1)} async-done(((bf16[256,1,1024]{2,0,1:T(8,128)(2,1)}), bf16[1024,1,1024]{2,0,1:T(8,128)(2,1)}) %all-gather.10.cloned.1.call-update) | async-done | bytes 2097168 | tf_op jit(solution)/shard_map/while/body/eval_jaxpr/all_gather | solution.py:155
  507.3 44.7 %reduce-scatter.8.cloned.1.call-done = f32[256,1,1024]{2,0,1:T(8,128)} async-done(((f32[1024,1,1024]{2,0,1:T(8,128)}), f32[256,1,1024]{2,0,1:T(8,128)}) %reduce-scatter.8.cloned.1.call-update) | async-done | bytes 1048592 | tf_op jit(solution)/shard_map/while/body/eval_jaxpr/reduce_scatter | solution.py:169
  555.3 22.2 %all-gather.12.cloned.1.call-done = bf16[1024,1,1024]{2,0,1:T(8,128)(2,1)} async-done(((bf16[256,1,1024]{2,0,1:T(8,128)(2,1)}), bf16[1024,1,1024]{2,0,1:T(8,128)(2,1)}) %all-gather.12.cloned.1.call-update) | async-done | bytes 2097168 | tf_op jit(solution)/shard_map/while/body/eval_jaxpr/all_gather | solution.py:178
  582.2 5.7 convert_reduce_fusion.9
  593.7 44.7 %reduce-scatter.12.cloned.1.call-done = f32[256,1,1024]{2,0,1:T(8,128)} async-done(((f32[1024,1,1024]{2,0,1:T(8,128)}), f32[256,1,1024]{2,0,1:T(8,128)}) %reduce-scatter.12.cloned.1.call-update) | async-done | bytes 1048592 | tf_op jit(solution)/shard_map/while/body/eval_jaxpr/reduce_scatter | solution.py:205
  642.9 7.0 convert_bitcast_fusion.4
  650.1 15.4 %all-gather.14.cloned.1.call-done = bf16[1024,1,1024]{2,0,1:T(8,128)(2,1)} async-done(((bf16[256,1,1024]{2,0,1:T(8,128)(2,1)}), bf16[1024,1,1024]{2,0,1:T(8,128)(2,1)}) %all-gather.14.cloned.1.call-update) | async-done | bytes 2097168 | tf_op jit(solution)/shard_map/while/body/eval_jaxpr/all_gather | solution.py:216
  673.0 7.6 multiply_reduce_fusion.13
  685.1 6.8 multiply_convert_fusion.11
  715.7 5.7 convolution_bitcast_fusion.8
  722.5 6.7 fusion.227
  749.2 10.1 %maximum_add_fusion.4 = f32[1024,3072]{0,1:T(8,128)} fusion(f32[1024,1024]{0,1:T(8,128)S(1)} %copy-done.11, f32[1024,1024]{0,1:T(8,128)S(1)} %copy-done.10, f32[1024,256]{0,1:T(8,128)S(1)} %fusion.228, f32[1024,768]{0,1:T(8,128)S(1)} %fusion.230, f32[1024,3072]{0,1:T(8,128)} %get-tuple-element.947, pred[]{:T(512)S(6)} %compare.3), kind=kLoop, calls=%fused_computation.clone.1 | loop fusion | flops 15728640 | bytes 37748736 | tf_op jit(solution)/shard_map/while/body/eval_jaxpr/add | solution.py:248
  759.3 7.1 reduce-scatter.14.cloned.1.call-done
  773.7 43.1 %psum.7 = f32[12288]{0:T(1024)S(1)} all-reduce(f32[12288]{0:T(1024)S(1)} %constant_dynamic-update-slice_fusion), channel_id=1, replica_groups=mesh['dp'=8,'tensor'=4] {'dp','tensor'}, use_global_device_ids=true, to_apply=%region_29.30 | all-reduce | flops 12288 | bytes 98304 | tf_op jit(solution)/shard_map/psum | solution.py:278
  818.7 167.7 %reduce-scatter.6.cloned.1.call-done = f32[128,3072]{0,1:T(8,128)} async-done(((f32[1024,3072]{0,1:T(8,128)}), f32[128,3072]{0,1:T(8,128)}) %reduce-scatter.6.cloned.1.call-update) | async-done | bytes 1572880 | tf_op jit(solution)/shard_map/reduce_scatter | solution.py:267
  (354 shorter events, 230.4 us)
Async XLA Ops:
  7.2 107.7 %all-gather.6.cloned.1.call-start = ((), (), s32[]{:S(2)}) async-start(), calls=%async_computation.5 | async-start | bytes 7077888 | tf_op jit(solution)/shard_map/all_gather | solution.py:125
  12.5 136.6 %all-gather.8.cloned.1.call-start = ((), (), s32[]{:S(2)}) async-start(), calls=%async_computation.6 | async-start | bytes 5242880 | tf_op jit(solution)/shard_map/all_gather | solution.py:131
  122.7 26.3 %copy-start.5 = (bf16[2,256,1,1024]{3,1,2,0:T(8,128)(2,1)S(1)}, bf16[2,256,1,1024]{3,1,2,0:T(8,128)(2,1)}, u32[]{:S(2)}) copy-start(bf16[2,256,1,1024]{3,1,2,0:T(8,128)(2,1)} %param.16) | copy-start | bytes 3145732
  122.7 26.3 %copy-start.20 = (f32[1024]{0:T(1024)S(1)}, f32[1024]{0:T(1024)}, u32[]{:S(2)}) copy-start(f32[1024]{0:T(1024)} %param.25) | copy-start | bytes 12292
  122.7 26.3 %copy-start.21 = (f32[1024]{0:T(1024)S(1)}, f32[1024]{0:T(1024)}, u32[]{:S(2)}) copy-start(f32[1024]{0:T(1024)} %param.27) | copy-start | bytes 12292
  122.7 26.3 %copy-start.22 = (f32[1024]{0:T(1024)S(1)}, f32[1024]{0:T(1024)}, u32[]{:S(2)}) copy-start(f32[1024]{0:T(1024)} %param.26) | copy-start | bytes 12292
  122.8 26.3 %copy-start.23 = (f32[1024]{0:T(1024)S(1)}, f32[1024]{0:T(1024)}, u32[]{:S(2)}) copy-start(f32[1024]{0:T(1024)} %param.20) | copy-start | bytes 12292
  122.8 26.3 %copy-start.24 = (f32[1024]{0:T(1024)S(1)}, f32[1024]{0:T(1024)}, u32[]{:S(2)}) copy-start(f32[1024]{0:T(1024)} %param.28) | copy-start | bytes 12292
  122.8 26.3 %copy-start.25 = (f32[1024]{0:T(1024)S(1)}, f32[1024]{0:T(1024)}, u32[]{:S(2)}) copy-start(f32[1024]{0:T(1024)} %param.24) | copy-start | bytes 12292
  122.8 26.3 %copy-start.26 = (f32[2,256]{1,0:T(2,128)S(1)}, f32[2,256]{1,0:T(2,128)}, u32[]{:S(2)}) copy-start(f32[2,256]{1,0:T(2,128)} %param.18) | copy-start | bytes 6148
  122.8 26.3 %copy-start.30 = (f32[1024]{0:T(1024)S(1)}, f32[1024]{0:T(1024)}, u32[]{:S(2)}) copy-start(f32[1024]{0:T(1024)} %param.22) | copy-start | bytes 12292
  149.4 43.9 %copy-start.16 = (bf16[1024,256]{1,0:T(8,128)(2,1)}, bf16[1024,256]{1,0:T(8,128)(2,1)S(1)}, u32[]{:S(2)}) copy-start(bf16[1024,256]{1,0:T(8,128)(2,1)S(1)} %get-tuple-element.992) | copy-start | bytes 1572868 | tf_op jit(solution)/shard_map/while
  149.4 25.5 %all-gather.10.cloned.1.call-start = ((), (), s32[]{:S(2)}) async-start(), calls=%async_computation.8 | async-start | bytes 2621440 | tf_op jit(solution)/shard_map/while/body/eval_jaxpr/all_gather | solution.py:155
  151.0 90.4 %reduce-scatter.8.cloned.1.call-start = ((), (), s32[]{:S(2)}) async-start(), calls=%async_computation.9 | async-start | bytes 5242880 | tf_op jit(solution)/shard_map/while/body/eval_jaxpr/reduce_scatter | solution.py:169
  196.6 70.3 %all-gather.12.cloned.1.call-start = ((), (), s32[]{:S(2)}) async-start(), calls=%async_computation.10 | async-start | bytes 2621440 | tf_op jit(solution)/shard_map/while/body/eval_jaxpr/all_gather | solution.py:178
  244.1 83.6 %reduce-scatter.12.cloned.1.call-start = ((), (), s32[]{:S(2)}) async-start(), calls=%async_computation.12 | async-start | bytes 5242880 | tf_op jit(solution)/shard_map/while/body/eval_jaxpr/reduce_scatter | solution.py:205
  283.0 71.9 %all-gather.14.cloned.1.call-start = ((), (), s32[]{:S(2)}) async-start(), calls=%async_computation.13 | async-start | bytes 2621440 | tf_op jit(solution)/shard_map/while/body/eval_jaxpr/all_gather | solution.py:216
  332.2 91.3 %reduce-scatter.10.cloned.1.call-start = ((), (), s32[]{:S(2)}) async-start(), calls=%async_computation.11 | async-start | bytes 2621440 | tf_op jit(solution)/shard_map/while/body/eval_jaxpr/reduce_scatter | solution.py:184
  339.3 116.5 %reduce-scatter.14.cloned.1.call-start = ((), (), s32[]{:S(2)}) async-start(), calls=%async_computation.14 | async-start | bytes 5242880 | tf_op jit(solution)/shard_map/while/body/eval_jaxpr/reduce_scatter | solution.py:234
  357.4 12.7 %slice-start.2 = ((s8[8388608]{0:T(1024)(128)(4,1)}), s8[4194304]{0:T(1024)(128)(4,1)S(1)}, s32[]{:S(2)}) async-start(s8[8388608]{0:T(1024)(128)(4,1)} %bitcast.324), calls=%async_computation.17 | async-start | bytes 8388608 | tf_op jit(solution)/shard_map/while
  444.2 15.8 %copy-start.17 = (bf16[1024,256]{1,0:T(8,128)(2,1)S(1)}, bf16[1024,256]{1,0:T(8,128)(2,1)}, u32[]{:S(2)}) copy-start(bf16[1024,256]{1,0:T(8,128)(2,1)} %copy-done.16) | copy-start | bytes 1572868 | tf_op jit(solution)/shard_map/while
  460.3 43.6 %copy-start.16 = (bf16[1024,256]{1,0:T(8,128)(2,1)}, bf16[1024,256]{1,0:T(8,128)(2,1)S(1)}, u32[]{:S(2)}) copy-start(bf16[1024,256]{1,0:T(8,128)(2,1)S(1)} %get-tuple-element.992) | copy-start | bytes 1572868 | tf_op jit(solution)/shard_map/while
  460.3 25.2 %all-gather.10.cloned.1.call-start = ((), (), s32[]{:S(2)}) async-start(), calls=%async_computation.8 | async-start | bytes 2621440 | tf_op jit(solution)/shard_map/while/body/eval_jaxpr/all_gather | solution.py:155
  461.9 90.1 %reduce-scatter.8.cloned.1.call-start = ((), (), s32[]{:S(2)}) async-start(), calls=%async_computation.9 | async-start | bytes 5242880 | tf_op jit(solution)/shard_map/while/body/eval_jaxpr/reduce_scatter | solution.py:169
  507.2 70.3 %all-gather.12.cloned.1.call-start = ((), (), s32[]{:S(2)}) async-start(), calls=%async_computation.10 | async-start | bytes 2621440 | tf_op jit(solution)/shard_map/while/body/eval_jaxpr/all_gather | solution.py:178
  554.8 83.6 %reduce-scatter.12.cloned.1.call-start = ((), (), s32[]{:S(2)}) async-start(), calls=%async_computation.12 | async-start | bytes 5242880 | tf_op jit(solution)/shard_map/while/body/eval_jaxpr/reduce_scatter | solution.py:205
  593.6 71.9 %all-gather.14.cloned.1.call-start = ((), (), s32[]{:S(2)}) async-start(), calls=%async_computation.13 | async-start | bytes 2621440 | tf_op jit(solution)/shard_map/while/body/eval_jaxpr/all_gather | solution.py:216
  642.8 91.3 %reduce-scatter.10.cloned.1.call-start = ((), (), s32[]{:S(2)}) async-start(), calls=%async_computation.11 | async-start | bytes 2621440 | tf_op jit(solution)/shard_map/while/body/eval_jaxpr/reduce_scatter | solution.py:184
  649.9 116.5 %reduce-scatter.14.cloned.1.call-start = ((), (), s32[]{:S(2)}) async-start(), calls=%async_computation.14 | async-start | bytes 5242880 | tf_op jit(solution)/shard_map/while/body/eval_jaxpr/reduce_scatter | solution.py:234
  668.0 12.7 %slice-start.2 = ((s8[8388608]{0:T(1024)(128)(4,1)}), s8[4194304]{0:T(1024)(128)(4,1)S(1)}, s32[]{:S(2)}) async-start(s8[8388608]{0:T(1024)(128)(4,1)} %bitcast.324), calls=%async_computation.17 | async-start | bytes 8388608 | tf_op jit(solution)/shard_map/while
  759.3 11.3 %copy-start.17 = (bf16[1024,256]{1,0:T(8,128)(2,1)S(1)}, bf16[1024,256]{1,0:T(8,128)(2,1)}, u32[]{:S(2)}) copy-start(bf16[1024,256]{1,0:T(8,128)(2,1)} %copy-done.16) | copy-start | bytes 1572868 | tf_op jit(solution)/shard_map/while
  772.8 213.5 %reduce-scatter.6.cloned.1.call-start = ((), (), s32[]{:S(2)}) async-start(), calls=%async_computation.7 | async-start | bytes 14155776 | tf_op jit(solution)/shard_map/reduce_scatter | solution.py:267
  (54 other events, 267.1 us)
Sparse Core Ops, SparseCore 0:
  12.6 102.1 all-gather.5
  116.4 32.6 all-gather.7
  152.3 22.5 all-gather.9
  196.7 44.5 reduce-scatter.7
  244.3 22.5 all-gather.11
  283.1 44.5 reduce-scatter.11
  332.3 22.5 all-gather.13
  357.4 31.1 reduce-scatter.9
  410.9 44.8 reduce-scatter.13
  462.9 22.5 all-gather.9
  507.3 44.5 reduce-scatter.7
  554.9 22.5 all-gather.11
  593.7 44.5 reduce-scatter.11
  642.9 22.5 all-gather.13
  667.9 31.1 reduce-scatter.9
  721.5 44.8 reduce-scatter.13
  776.9 209.3 reduce-scatter.5
where the time goes:
time: 1000 us; the launch traced here: 999 us
  waiting for transfers between devices  608 us (61%)
  matrix products  180 us (18%)
  other arithmetic  85.3 us (9%)
  local copies, waits for them, and re-layouts  62.5 us (6%)
  blocking collectives  43.1 us (4%)
  between operations  14.7 us (1%)
    reduce_scatter x1, waiting for transfers between devices, per_device(): lax.psum_scatter(weight_acc, 'dp', scatter_dimension=0, tiled=True)  168 us
    all_gather x1, waiting for transfers between devices, per_device(): packed_full = lax.all_gather(packed, 'dp', axis=0, tiled=True)  101 us
    reduce_scatter x2, waiting for transfers between devices, one_micro(): lax.psum_scatter(jnp.einsum('lbi,oi->lbo', mixed, out_full, preferred_ele...  89.4 us
    reduce_scatter x2, waiting for transfers between devices, one_micro(): lax.psum_scatter(jnp.einsum('lbf,df->lbd', grad_pre, fc_full, preferred_e...  89.3 us
    all_gather x2, waiting for transfers between devices, one_micro(): hidden1_full = lax.all_gather(hidden1, 'tensor', axis=0, tiled=True)  46.1 us
    all_gather x2, waiting for transfers between devices, one_micro(): hidden2_full = lax.all_gather(hidden2, 'tensor', axis=0, tiled=True)  44.6 us
    psum x1, blocking collectives, per_device(): lax.psum(jnp.concatenate([feature_vec, head_slots.reshape(-1)]), ('dp', '...  43.1 us
    all_gather x2, waiting for transfers between devices, one_micro(): lax.all_gather(grad_mid.astype(jnp.bfloat16), 'tensor', axis=0, tiled=True)  30.5 us
  transfers between devices with their start and end apart: 17, of which 15 were waited for; matrix products, arithmetic and copies ran while one was open for 21% of the time, Pallas kernels for 0%

commit v1 on v0

--- a/solution.py
+++ b/solution.py
@@ -112,6 +112,34 @@
     norm2_shift,
     out_grad,
 ):
+
+    def classes_load(own_rows, a_name, dim_k):
+        x_now = lax.axis_index(a_name)
+        passed = lax.axis_size(a_name)
+        left_arr, local_out, field_out = (passed, x_now, own_rows.shape[dim_k])
+        vals = [(pp, (pp + 1) % left_arr) for pp in range(left_arr)]
+        sides = [(pp, (pp - 1) % left_arr) for pp in range(left_arr)]
+        high = jnp.zeros(
+            (*own_rows.shape[:dim_k], left_arr * field_out, *own_rows.shape[dim_k + 1 :]),
+            own_rows.dtype,
+        )
+        r_now = placed = own_rows
+        step_out = left_arr // 2
+        kk = 1
+        high = lax.dynamic_update_slice_in_dim(high, own_rows, local_out * field_out, axis=dim_k)
+        while kk < step_out + 1:
+            r_now = lax.ppermute(r_now, a_name, vals)
+            high = lax.dynamic_update_slice_in_dim(
+                high, r_now, (local_out - kk) % left_arr * field_out, axis=dim_k
+            )
+            if kk < left_arr - step_out:
+                placed = lax.ppermute(placed, a_name, sides)
+                high = lax.dynamic_update_slice_in_dim(
+                    high, placed, (local_out + kk) % left_arr * field_out, axis=dim_k
+                )
+            kk = kk + 1
+        return high
+
     micro = block_input.shape[0]
     heads_local = qkv_weight.shape[2] // HEAD_DIM
     rows = qkv_weight.shape[0]
@@ -122,7 +150,7 @@
     packed = jnp.concatenate(
         [qkv_weight.reshape(rows, width_qkv), out_weight, fc_weight, proj_weight], axis=1
     )
-    packed_full = lax.all_gather(packed, "dp", axis=0, tiled=True)
+    packed_full = classes_load(packed, "dp", 0)
     depth = packed_full.shape[0]
     qkv_full = packed_full[:, : cuts[0]].reshape(depth, 3, qkv_weight.shape[2])
     out_full = packed_full[:, cuts[0] : cuts[1]]

time: 1000 us -> 1020 us (1.020)
  waiting for transfers between devices: 608 us -> 588 us
  starting transfers between devices: 2.08 us -> 21.8 us
  local copies, waits for them, and re-layouts: 62.5 us -> 74.9 us
    ppermute x0 -> x7, waiting for transfers between devices: none -> 102 us  [the longest x4 86.1 us: classes_load(): r_now = lax.ppermute(r_now, a_name, vals)]
    all_gather x1 -> x0, waiting for transfers between devices: 101 us -> none  [per_device(): packed_full = lax.all_gather(packed, 'dp', axis=0, tiled=True)]
    ppermute x0 -> x7, starting transfers between devices: none -> 19.7 us  [the longest x4 10.4 us: classes_load(): r_now = lax.ppermute(r_now, a_name, vals)]
    all_gather x1, waiting for transfers between devices: 19 us -> 0.01 us  [per_device(): grad_top_all = lax.all_gather(out_grad, 'tensor', axis=1, tiled=True)]
  transfers between devices with their start and end apart: 17 -> 23, of which waited for: 15 -> 17; matrix products, arithmetic and copies ran while one was open for 21% -> 22% of each run, Pallas kernels for 0% -> 0%
where the time goes in v1:
time: 1020 us; the launch traced here: 1010 us
  waiting for transfers between devices  588 us (58%)
  matrix products  180 us (18%)
  other arithmetic  85.3 us (8%)
  local copies, waits for them, and re-layouts  74.9 us (7%)
  blocking collectives  43 us (4%)
  starting transfers between devices  21.8 us (2%)
  between operations  14.7 us (1%)
    reduce_scatter x1, waiting for transfers between devices, per_device(): lax.psum_scatter(weight_acc, 'dp', scatter_dimension=0, tiled=True)  168 us
    reduce_scatter x2, waiting for transfers between devices, one_micro(): lax.psum_scatter(jnp.einsum('lbi,oi->lbo', mixed, out_full, preferred_ele...  89.4 us
    reduce_scatter x2, waiting for transfers between devices, one_micro(): lax.psum_scatter(jnp.einsum('lbf,df->lbd', grad_pre, fc_full, preferred_e...  89.3 us
    ppermute x4, waiting for transfers between devices, classes_load(): r_now = lax.ppermute(r_now, a_name, vals)  86.1 us
    all_gather x2, waiting for transfers between devices, one_micro(): hidden2_full = lax.all_gather(hidden2, 'tensor', axis=0, tiled=True)  44.6 us
    all_gather x2, waiting for transfers between devices, one_micro(): hidden1_full = lax.all_gather(hidden1, 'tensor', axis=0, tiled=True)  43.8 us
    psum x1, blocking collectives, per_device(): lax.psum(jnp.concatenate([feature_vec, head_slots.reshape(-1)]), ('dp', '...  43 us
    all_gather x2, waiting for transfers between devices, one_micro(): lax.all_gather(grad_mid.astype(jnp.bfloat16), 'tensor', axis=0, tiled=True)  30.5 us
  transfers between devices with their start and end apart: 23, of which 17 were waited for; matrix products, arithmetic and copies ran while one was open for 22% of the time, Pallas kernels for 0%

profile of v1, /device:TPU:0, one launch (start us, length us, event | category | flops | bytes accessed | tf_op | source)
XLA Modules:
  0.0 1010.9 jit_solution(15744067232532264027)
XLA Ops:
  22.8 30.6 %collective-permute-done = bf16[128,3072]{0,1:T(8,128)(2,1)S(1)} collective-permute-done((bf16[128,3072]{0,1:T(8,128)(2,1)S(1)}, bf16[128,3072]{0,1:T(8,128)(2,1)S(1)}, u32[]{:S(2)}, u32[]{:S(2)}) %collective-permute-start) | collective-permute-done | bytes 786464 | tf_op jit(solution)/shard_map/ppermute | solution.py:131
  59.0 29.6 %collective-permute-done.2 = bf16[128,3072]{0,1:T(8,128)(2,1)S(1)} collective-permute-done((bf16[128,3072]{0,1:T(8,128)(2,1)S(1)}, bf16[128,3072]{0,1:T(8,128)(2,1)S(1)}, u32[]{:S(2)}, u32[]{:S(2)}) %collective-permute-start.2) | collective-permute-done | bytes 786464 | tf_op jit(solution)/shard_map/ppermute | solution.py:131
  97.3 25.9 %collective-permute-done.4 = bf16[128,3072]{0,1:T(8,128)(2,1)S(1)} collective-permute-done((bf16[128,3072]{0,1:T(8,128)(2,1)S(1)}, bf16[128,3072]{0,1:T(8,128)(2,1)S(1)}, u32[]{:S(2)}, u32[]{:S(2)}) %collective-permute-start.4) | collective-permute-done | bytes 786464 | tf_op jit(solution)/shard_map/ppermute | solution.py:131
  127.6 16.1 %collective-permute-done.5 = bf16[128,3072]{0,1:T(8,128)(2,1)S(1)} collective-permute-done((bf16[128,3072]{0,1:T(8,128)(2,1)S(1)}, bf16[128,3072]{0,1:T(8,128)(2,1)S(1)}, u32[]{:S(2)}, u32[]{:S(2)}) %collective-permute-start.5) | collective-permute-done | bytes 786464 | tf_op jit(solution)/shard_map/ppermute | solution.py:136
  163.0 621.4 %while.34 = (s32[]{:T(128)}, bf16[2,256,1,1024]{3,1,2,0:T(8,128)(2,1)}, bf16[2,256,1,1024]{3,1,2,0:T(8,128)(2,1)}, f32[1024,3072]{0,1:T(8,128)}, f32[2,256]{1,0:...) while((s32[]{:T(128)}, ...), condition=%wide.region_27.28_spmd.clone, body=%wide.region_0.27_spmd.clone.sunk | while | flops 22718711808 | bytes 744419392 | solution.py:292
  165.6 20.6 %all-gather.7.cloned.1.call-done = bf16[1024,1,1024]{2,0,1:T(8,128)(2,1)} async-done(((bf16[256,1,1024]{2,0,1:T(8,128)(2,1)}), bf16[1024,1,1024]{2,0,1:T(8,128)(2,1)}) %all-gather.7.cloned.1.call-update) | async-done | bytes 2097168 | tf_op jit(solution)/shard_map/while/body/eval_jaxpr/all_gather | solution.py:183
  208.0 44.7 %reduce-scatter.8.cloned.1.call-done = f32[256,1,1024]{2,0,1:T(8,128)} async-done(((f32[1024,1,1024]{2,0,1:T(8,128)}), f32[256,1,1024]{2,0,1:T(8,128)}) %reduce-scatter.8.cloned.1.call-update) | async-done | bytes 1048592 | tf_op jit(solution)/shard_map/while/body/eval_jaxpr/reduce_scatter | solution.py:197
  255.7 22.4 %all-gather.9.cloned.1.call-done = bf16[1024,1,1024]{2,0,1:T(8,128)(2,1)} async-done(((bf16[256,1,1024]{2,0,1:T(8,128)(2,1)}), bf16[1024,1,1024]{2,0,1:T(8,128)(2,1)}) %all-gather.9.cloned.1.call-update) | async-done | bytes 2097168 | tf_op jit(solution)/shard_map/while/body/eval_jaxpr/all_gather | solution.py:206
  282.9 5.7 convert_reduce_fusion.9
  294.4 44.7 %reduce-scatter.12.cloned.1.call-done = f32[256,1,1024]{2,0,1:T(8,128)} async-done(((f32[1024,1,1024]{2,0,1:T(8,128)}), f32[256,1,1024]{2,0,1:T(8,128)}) %reduce-scatter.12.cloned.1.call-update) | async-done | bytes 1048592 | tf_op jit(solution)/shard_map/while/body/eval_jaxpr/reduce_scatter | solution.py:233
  343.6 7.0 convert_bitcast_fusion.4
  351.1 15.1 %all-gather.11.cloned.1.call-done = bf16[1024,1,1024]{2,0,1:T(8,128)(2,1)} async-done(((bf16[256,1,1024]{2,0,1:T(8,128)(2,1)}), bf16[1024,1,1024]{2,0,1:T(8,128)(2,1)}) %all-gather.11.cloned.1.call-update) | async-done | bytes 2097168 | tf_op jit(solution)/shard_map/while/body/eval_jaxpr/all_gather | solution.py:244
  373.7 7.6 multiply_reduce_fusion.13
  385.9 6.8 multiply_convert_fusion.11
  416.3 5.6 convolution_bitcast_fusion.8
  423.2 6.7 fusion.228
  455.4 11.7 %reduce-scatter.14.cloned.1.call-done = f32[256,1,1024]{2,0,1:T(8,128)} async-done(((f32[1024,1,1024]{2,0,1:T(8,128)}), f32[256,1,1024]{2,0,1:T(8,128)}) %reduce-scatter.14.cloned.1.call-update) | async-done | bytes 1048592 | tf_op jit(solution)/shard_map/while/body/eval_jaxpr/reduce_scatter | solution.py:262
  473.9 23.2 %all-gather.7.cloned.1.call-done = bf16[1024,1,1024]{2,0,1:T(8,128)(2,1)} async-done(((bf16[256,1,1024]{2,0,1:T(8,128)(2,1)}), bf16[1024,1,1024]{2,0,1:T(8,128)(2,1)}) %all-gather.7.cloned.1.call-update) | async-done | bytes 2097168 | tf_op jit(solution)/shard_map/while/body/eval_jaxpr/all_gather | solution.py:183
  518.8 44.7 %reduce-scatter.8.cloned.1.call-done = f32[256,1,1024]{2,0,1:T(8,128)} async-done(((f32[1024,1,1024]{2,0,1:T(8,128)}), f32[256,1,1024]{2,0,1:T(8,128)}) %reduce-scatter.8.cloned.1.call-update) | async-done | bytes 1048592 | tf_op jit(solution)/shard_map/while/body/eval_jaxpr/reduce_scatter | solution.py:197
  566.9 22.2 %all-gather.9.cloned.1.call-done = bf16[1024,1,1024]{2,0,1:T(8,128)(2,1)} async-done(((bf16[256,1,1024]{2,0,1:T(8,128)(2,1)}), bf16[1024,1,1024]{2,0,1:T(8,128)(2,1)}) %all-gather.9.cloned.1.call-update) | async-done | bytes 2097168 | tf_op jit(solution)/shard_map/while/body/eval_jaxpr/all_gather | solution.py:206
  593.8 5.7 convert_reduce_fusion.9
  605.3 44.7 %reduce-scatter.12.cloned.1.call-done = f32[256,1,1024]{2,0,1:T(8,128)} async-done(((f32[1024,1,1024]{2,0,1:T(8,128)}), f32[256,1,1024]{2,0,1:T(8,128)}) %reduce-scatter.12.cloned.1.call-update) | async-done | bytes 1048592 | tf_op jit(solution)/shard_map/while/body/eval_jaxpr/reduce_scatter | solution.py:233
  654.5 7.0 convert_bitcast_fusion.4
  661.7 15.4 %all-gather.11.cloned.1.call-done = bf16[1024,1,1024]{2,0,1:T(8,128)(2,1)} async-done(((bf16[256,1,1024]{2,0,1:T(8,128)(2,1)}), bf16[1024,1,1024]{2,0,1:T(8,128)(2,1)}) %all-gather.11.cloned.1.call-update) | async-done | bytes 2097168 | tf_op jit(solution)/shard_map/while/body/eval_jaxpr/all_gather | solution.py:244
  684.6 7.6 multiply_reduce_fusion.13
  696.7 6.8 multiply_convert_fusion.11
  727.2 5.6 convolution_bitcast_fusion.8
  734.1 6.7 fusion.228
  760.7 10.1 maximum_add_fusion.4
  770.8 7.2 reduce-scatter.14.cloned.1.call-done
  785.3 43.0 %psum.7 = f32[12288]{0:T(1024)S(1)} all-reduce(f32[12288]{0:T(1024)S(1)} %constant_dynamic-update-slice_fusion), channel_id=1, replica_groups=mesh['dp'=8,'tensor'=4] {'dp','tensor'}, use_global_device_ids=true, to_apply=%region_29.30 | all-reduce | flops 12288 | bytes 98304 | tf_op jit(solution)/shard_map/psum | solution.py:306
  830.2 167.7 %reduce-scatter.6.cloned.1.call-done = f32[128,3072]{0,1:T(8,128)} async-done(((f32[1024,3072]{0,1:T(8,128)}), f32[128,3072]{0,1:T(8,128)}) %reduce-scatter.6.cloned.1.call-update) | async-done | bytes 1572880 | tf_op jit(solution)/shard_map/reduce_scatter | solution.py:295
  (372 shorter events, 273.7 us)
Async XLA Ops:
  7.2 155.7 %all-gather.5.cloned.1.call-start = ((), (), s32[]{:S(2)}) async-start(), calls=%async_computation.5 | async-start | bytes 5242880 | tf_op jit(solution)/shard_map/all_gather | solution.py:159
  16.7 36.6 %collective-permute-start = (bf16[128,3072]{0,1:T(8,128)(2,1)S(1)}, bf16[128,3072]{0,1:T(8,128)(2,1)S(1)}, u32[]{:S(2)}, u32[]{:S(2)}) collective-permute-start(bf16[128,3072]{0,1:T(8,128)(2,1)S(1)} %get-tuple-element.676), channel_id=1, source_target_pairs={{0,4},{4,8},{8,12},{12,16},{16,20},{20,24},{24,28},{28,0},{1,5},{5... | collective-permute-start | bytes 2359304 | tf_op jit(solution)/shard_map/ppermute | solution.py:131
  19.7 36.1 %collective-permute-start.1 = (bf16[128,3072]{0,1:T(8,128)(2,1)S(1)}, bf16[128,3072]{0,1:T(8,128)(2,1)S(1)}, u32[]{:S(2)}, u32[]{:S(2)}) collective-permute-start(bf16[128,3072]{0,1:T(8,128)(2,1)S(1)} %get-tuple-element.676), channel_id=1, source_target_pairs={{0,28},{4,0},{8,4},{12,8},{16,12},{20,16},{24,20},{28,24},{1,29},{... | collective-permute-start | bytes 2359304 | tf_op jit(solution)/shard_map/ppermute | solution.py:136
  53.3 35.3 %collective-permute-start.2 = (bf16[128,3072]{0,1:T(8,128)(2,1)S(1)}, bf16[128,3072]{0,1:T(8,128)(2,1)S(1)}, u32[]{:S(2)}, u32[]{:S(2)}) collective-permute-start(bf16[128,3072]{0,1:T(8,128)(2,1)S(1)} %collective-permute-done), channel_id=1, source_target_pairs={{0,4},{4,8},{8,12},{12,16},{16,20},{20,24},{24,28},{28,0},{1,5},{5... | collective-permute-start | bytes 2359304 | tf_op jit(solution)/shard_map/ppermute | solution.py:131
  55.8 37.3 %collective-permute-start.3 = (bf16[128,3072]{0,1:T(8,128)(2,1)S(1)}, bf16[128,3072]{0,1:T(8,128)(2,1)S(1)}, u32[]{:S(2)}, u32[]{:S(2)}) collective-permute-start(bf16[128,3072]{0,1:T(8,128)(2,1)S(1)} %collective-permute-done.1), channel_id=1, source_target_pairs={{0,28},{4,0},{8,4},{12,8},{16,12},{20,16},{24,20},{28,24},{1,29},{... | collective-permute-start | bytes 2359304 | tf_op jit(solution)/shard_map/ppermute | solution.py:136
  88.6 34.6 %collective-permute-start.4 = (bf16[128,3072]{0,1:T(8,128)(2,1)S(1)}, bf16[128,3072]{0,1:T(8,128)(2,1)S(1)}, u32[]{:S(2)}, u32[]{:S(2)}) collective-permute-start(bf16[128,3072]{0,1:T(8,128)(2,1)S(1)} %collective-permute-done.2), channel_id=1, source_target_pairs={{0,4},{4,8},{8,12},{12,16},{16,20},{20,24},{24,28},{28,0},{1,5},{5... | collective-permute-start | bytes 2359304 | tf_op jit(solution)/shard_map/ppermute | solution.py:131
  93.1 50.6 %collective-permute-start.5 = (bf16[128,3072]{0,1:T(8,128)(2,1)S(1)}, bf16[128,3072]{0,1:T(8,128)(2,1)S(1)}, u32[]{:S(2)}, u32[]{:S(2)}) collective-permute-start(bf16[128,3072]{0,1:T(8,128)(2,1)S(1)} %collective-permute-done.3), channel_id=1, source_target_pairs={{0,28},{4,0},{8,4},{12,8},{16,12},{20,16},{24,20},{28,24},{1,29},{... | collective-permute-start | bytes 2359304 | tf_op jit(solution)/shard_map/ppermute | solution.py:136
  123.2 21.5 %collective-permute-start.6 = (bf16[128,3072]{0,1:T(8,128)(2,1)S(1)}, bf16[128,3072]{0,1:T(8,128)(2,1)S(1)}, u32[]{:S(2)}, u32[]{:S(2)}) collective-permute-start(bf16[128,3072]{0,1:T(8,128)(2,1)S(1)} %collective-permute-done.4), channel_id=1, source_target_pairs={{0,4},{4,8},{8,12},{12,16},{16,20},{20,24},{24,28},{28,0},{1,5},{5... | collective-permute-start | bytes 2359304 | tf_op jit(solution)/shard_map/ppermute | solution.py:131
  163.2 41.3 %copy-start.16 = (bf16[1024,256]{1,0:T(8,128)(2,1)}, bf16[1024,256]{1,0:T(8,128)(2,1)S(1)}, u32[]{:S(2)}) copy-start(bf16[1024,256]{1,0:T(8,128)(2,1)S(1)} %get-tuple-element.994) | copy-start | bytes 1572868 | tf_op jit(solution)/shard_map/while
  163.2 23.0 %all-gather.7.cloned.1.call-start = ((), (), s32[]{:S(2)}) async-start(), calls=%async_computation.7 | async-start | bytes 2621440 | tf_op jit(solution)/shard_map/while/body/eval_jaxpr/all_gather | solution.py:183
  164.8 87.8 %reduce-scatter.8.cloned.1.call-start = ((), (), s32[]{:S(2)}) async-start(), calls=%async_computation.8 | async-start | bytes 5242880 | tf_op jit(solution)/shard_map/while/body/eval_jaxpr/reduce_scatter | solution.py:197
  190.1 10.9 %copy-start.7 = (bf16[1024,3,256]{0,2,1:T(8,128)(2,1)}, bf16[1024,3,256]{0,2,1:T(8,128)(2,1)S(1)}, u32[]{:S(2)}) copy-start(bf16[1024,3,256]{0,2,1:T(8,128)(2,1)S(1)} %add_convert_fusion.5) | copy-start | bytes 4718596 | tf_op jit(solution)/shard_map/while
  207.9 70.3 %all-gather.9.cloned.1.call-start = ((), (), s32[]{:S(2)}) async-start(), calls=%async_computation.9 | async-start | bytes 2621440 | tf_op jit(solution)/shard_map/while/body/eval_jaxpr/all_gather | solution.py:206
  255.4 83.6 %reduce-scatter.12.cloned.1.call-start = ((), (), s32[]{:S(2)}) async-start(), calls=%async_computation.11 | async-start | bytes 5242880 | tf_op jit(solution)/shard_map/while/body/eval_jaxpr/reduce_scatter | solution.py:233
  294.3 71.9 %all-gather.11.cloned.1.call-start = ((), (), s32[]{:S(2)}) async-start(), calls=%async_computation.12 | async-start | bytes 2621440 | tf_op jit(solution)/shard_map/while/body/eval_jaxpr/all_gather | solution.py:244
  343.5 91.2 %reduce-scatter.10.cloned.1.call-start = ((), (), s32[]{:S(2)}) async-start(), calls=%async_computation.10 | async-start | bytes 2621440 | tf_op jit(solution)/shard_map/while/body/eval_jaxpr/reduce_scatter | solution.py:212
  350.6 116.5 %reduce-scatter.14.cloned.1.call-start = ((), (), s32[]{:S(2)}) async-start(), calls=%async_computation.13 | async-start | bytes 5242880 | tf_op jit(solution)/shard_map/while/body/eval_jaxpr/reduce_scatter | solution.py:262
  368.7 12.6 %slice-start.2 = ((s8[8388608]{0:T(1024)(128)(4,1)}), s8[4194304]{0:T(1024)(128)(4,1)S(1)}, s32[]{:S(2)}) async-start(s8[8388608]{0:T(1024)(128)(4,1)} %bitcast.324), calls=%async_computation.16 | async-start | bytes 8388608 | tf_op jit(solution)/shard_map/while
  385.9 8.8 copy-start.8
  455.4 15.9 %copy-start.17 = (bf16[1024,256]{1,0:T(8,128)(2,1)S(1)}, bf16[1024,256]{1,0:T(8,128)(2,1)}, u32[]{:S(2)}) copy-start(bf16[1024,256]{1,0:T(8,128)(2,1)} %copy-done.16) | copy-start | bytes 1572868 | tf_op jit(solution)/shard_map/while
  471.5 43.9 %copy-start.16 = (bf16[1024,256]{1,0:T(8,128)(2,1)}, bf16[1024,256]{1,0:T(8,128)(2,1)S(1)}, u32[]{:S(2)}) copy-start(bf16[1024,256]{1,0:T(8,128)(2,1)S(1)} %get-tuple-element.994) | copy-start | bytes 1572868 | tf_op jit(solution)/shard_map/while
  471.5 25.5 %all-gather.7.cloned.1.call-start = ((), (), s32[]{:S(2)}) async-start(), calls=%async_computation.7 | async-start | bytes 2621440 | tf_op jit(solution)/shard_map/while/body/eval_jaxpr/all_gather | solution.py:183
  473.2 90.4 %reduce-scatter.8.cloned.1.call-start = ((), (), s32[]{:S(2)}) async-start(), calls=%async_computation.8 | async-start | bytes 5242880 | tf_op jit(solution)/shard_map/while/body/eval_jaxpr/reduce_scatter | solution.py:197
  501.0 10.9 %copy-start.7 = (bf16[1024,3,256]{0,2,1:T(8,128)(2,1)}, bf16[1024,3,256]{0,2,1:T(8,128)(2,1)S(1)}, u32[]{:S(2)}) copy-start(bf16[1024,3,256]{0,2,1:T(8,128)(2,1)S(1)} %add_convert_fusion.5) | copy-start | bytes 4718596 | tf_op jit(solution)/shard_map/while
  518.8 70.3 %all-gather.9.cloned.1.call-start = ((), (), s32[]{:S(2)}) async-start(), calls=%async_computation.9 | async-start | bytes 2621440 | tf_op jit(solution)/shard_map/while/body/eval_jaxpr/all_gather | solution.py:206
  566.3 83.6 %reduce-scatter.12.cloned.1.call-start = ((), (), s32[]{:S(2)}) async-start(), calls=%async_computation.11 | async-start | bytes 5242880 | tf_op jit(solution)/shard_map/while/body/eval_jaxpr/reduce_scatter | solution.py:233
  605.2 71.9 %all-gather.11.cloned.1.call-start = ((), (), s32[]{:S(2)}) async-start(), calls=%async_computation.12 | async-start | bytes 2621440 | tf_op jit(solution)/shard_map/while/body/eval_jaxpr/all_gather | solution.py:244
  654.4 91.3 %reduce-scatter.10.cloned.1.call-start = ((), (), s32[]{:S(2)}) async-start(), calls=%async_computation.10 | async-start | bytes 2621440 | tf_op jit(solution)/shard_map/while/body/eval_jaxpr/reduce_scatter | solution.py:212
  661.5 116.5 %reduce-scatter.14.cloned.1.call-start = ((), (), s32[]{:S(2)}) async-start(), calls=%async_computation.13 | async-start | bytes 5242880 | tf_op jit(solution)/shard_map/while/body/eval_jaxpr/reduce_scatter | solution.py:262
  679.6 12.6 %slice-start.2 = ((s8[8388608]{0:T(1024)(128)(4,1)}), s8[4194304]{0:T(1024)(128)(4,1)S(1)}, s32[]{:S(2)}) async-start(s8[8388608]{0:T(1024)(128)(4,1)} %bitcast.324), calls=%async_computation.16 | async-start | bytes 8388608 | tf_op jit(solution)/shard_map/while
  770.8 11.4 %copy-start.17 = (bf16[1024,256]{1,0:T(8,128)(2,1)S(1)}, bf16[1024,256]{1,0:T(8,128)(2,1)}, u32[]{:S(2)}) copy-start(bf16[1024,256]{1,0:T(8,128)(2,1)} %copy-done.16) | copy-start | bytes 1572868 | tf_op jit(solution)/shard_map/while
  784.4 213.5 %reduce-scatter.6.cloned.1.call-start = ((), (), s32[]{:S(2)}) async-start(), calls=%async_computation.6 | async-start | bytes 14155776 | tf_op jit(solution)/shard_map/reduce_scatter | solution.py:295
  (59 other events, 294.6 us)
Sparse Core Ops, SparseCore 0:
  9.5 37.1 all-gather.4
  166.2 19.9 all-gather.6
  208.0 44.5 reduce-scatter.7
  255.5 22.5 all-gather.8
  294.4 44.5 reduce-scatter.11
  343.6 22.5 all-gather.10
  368.7 31.1 reduce-scatter.9
  422.1 44.9 reduce-scatter.13
  474.5 22.5 all-gather.6
  518.9 44.5 reduce-scatter.7
  566.5 22.5 all-gather.8
  605.3 44.5 reduce-scatter.11
  654.5 22.5 all-gather.10
  679.5 31.1 reduce-scatter.9
  733.0 44.8 reduce-scatter.13
  788.5 209.3 reduce-scatter.5
